TPU v7x, 256 devices: a whole 4x4x8 slice. The times are simulated.
256 devices in a mesh: lat: 16 (over z, core), lon: 16 (over y, x).
Axes of the slice: x: 4, y: 4, z: 8, core: 2. Of those that a mesh axis runs over, the one named last changes fastest.
Arguments:
- predicted_state: float32 [1440, 26624], P('lon', 'lat'), may hold values from -24 to 24
- verified_state: float32 [1440, 26624], P('lon', 'lat'), may hold values from -20 to 20
- normal_state: float32 [1440, 26624], P('lon', 'lat'), may hold values from -3 to 3
Outputs:
- energy_curves: float32 [3, 52, 721], replicated
- rms_error: float32 [52], replicated
- anomaly_corr: float32 [52], replicated
All inputs are finite; a program needn't handle non-finite values.
Results may differ from a plain program's by a relative error of at most 0.00005.
Values sent between devices are 32-bit elements; how exact they have to be, the bound alone decides.
No kernel may reach another device: no remote copies, remote signals or barrier semaphores. Data moves between devices by JAX's collectives and lax.ppermute only.
A program may use at most 64 MiB of HBM per device.

v0:
```python
import jax
import jax.numpy as jnp
from jax import lax
from jax.sharding import Mesh
from jax.sharding import PartitionSpec as P

FIELDS = 52
LAT = ("lat_0", "lat_1")
LON = ("lon_0", "lon_1")
LAT_LON = ("lat_0", "lat_1", "lon_0", "lon_1")


epsilon = 1e-06


def gathered_total(value, axis):
    tiles = lax.all_gather(value, axis)
    return tiles.sum(axis=0)


def copy_for_each(value, axis):
    copies = jnp.broadcast_to(value, (lax.axis_size(axis), *value.shape))
    return lax.all_to_all(copies, axis, split_axis=0, concat_axis=0, tiled=True)


def in_order(tiles, dim):
    lengths = list(tiles.shape[1:])
    lengths[dim] *= tiles.shape[0]
    return jnp.moveaxis(tiles, 0, dim).reshape(lengths)


def gather_directly(value, axis, dim):
    tiles = copy_for_each(value, axis)
    return in_order(tiles, dim)


def one_axis_at_a_time(value, axes):
    for axis in axes:
        value = lax.psum(value, axis)
    return value


def latitude_weights(lat_index, parallel_number):
    return jnp.cos(jnp.pi * ((lat_index.astype(jnp.float32) + 0.5) / parallel_number - 0.5))


def dft_table(lon_rows, lon_total, wave_count):
    longitudes = jnp.arange(lon_rows, dtype=jnp.int32)
    waves = jnp.arange(wave_count, dtype=jnp.int32)
    phase = longitudes[:, None] * waves[None, :] % lon_total
    angle = 2.0 * jnp.pi / lon_total * phase.astype(jnp.float32)
    return jnp.concatenate([jnp.cos(angle), -jnp.sin(angle)], axis=1)


def transform_columns(stacked, table):
    return lax.dot_general(
        stacked,
        table,
        (((0,), (0,)), ((), ())),
        precision=lax.Precision.HIGHEST,
        preferred_element_type=jnp.float32,
    )


def row_powers(fore_coeffs, true_coeffs, wave_count):
    diff_coeffs = fore_coeffs - true_coeffs

    def square(coeffs):
        return (
            coeffs[:, :wave_count] * coeffs[:, :wave_count]
            + coeffs[:, wave_count:] * coeffs[:, wave_count:]
        )

    return jnp.stack([square(fore_coeffs), square(true_coeffs), square(diff_coeffs)], axis=1)


def local(predicted_state, verified_state, normal_state):
    quantity_labels = FIELDS
    meridian_lines, meridian_number = predicted_state.shape
    parallel_lines = meridian_number // quantity_labels
    parallel_number = parallel_lines * lax.axis_size(LAT)
    lon_devices = lax.axis_size(LON)
    lon_total = meridian_lines * lon_devices
    wave_count = lon_total // 2 + 1
    row_share = meridian_number // lon_devices
    lat_first = lax.axis_index(LAT) * parallel_lines
    weights = latitude_weights(
        lat_first + jnp.arange(parallel_lines, dtype=jnp.int32), parallel_number
    )
    weight_total = jnp.sum(
        latitude_weights(jnp.arange(parallel_number, dtype=jnp.int32), parallel_number)
    )
    predicted_block = predicted_state.reshape(meridian_lines, parallel_lines, quantity_labels)
    observed_block = verified_state.reshape(meridian_lines, parallel_lines, quantity_labels)
    normal_block = normal_state.reshape(meridian_lines, parallel_lines, quantity_labels)
    mismatch_parts = predicted_block - observed_block
    predicted_anomalies = predicted_block - normal_block
    observed_anomalies = observed_block - normal_block
    broad_layout = weights[None, :, None]
    skill_terms = jnp.stack(
        [
            jnp.sum(broad_layout * mismatch_parts * mismatch_parts, axis=(0, 1)),
            jnp.sum(broad_layout * predicted_anomalies * observed_anomalies, axis=(0, 1)),
            jnp.sum(broad_layout * predicted_anomalies * predicted_anomalies, axis=(0, 1)),
            jnp.sum(broad_layout * observed_anomalies * observed_anomalies, axis=(0, 1)),
        ]
    )
    predicted_meridians = predicted_block.transpose(0, 2, 1).reshape(
        meridian_lines, meridian_number
    )
    true_cols = observed_block.transpose(0, 2, 1).reshape(meridian_lines, meridian_number)
    full_table = dft_table(lon_total, lon_total, wave_count)
    fore_blocks = predicted_meridians.reshape(meridian_lines, lon_devices, row_share)
    true_blocks = true_cols.reshape(meridian_lines, lon_devices, row_share)
    fore_part = lax.all_to_all(fore_blocks, LON, split_axis=1, concat_axis=0, tiled=True)[:, 0, :]
    true_part = lax.all_to_all(true_blocks, LON, split_axis=1, concat_axis=0, tiled=True)[:, 0, :]
    items = fore_part.shape[1]
    stacked = jnp.concatenate([fore_part, true_part], axis=1)
    coeffs = transform_columns(stacked, full_table)
    powers = row_powers(coeffs[:items], coeffs[items:], wave_count)
    share_start = lax.axis_index(LON) * row_share
    global_cols = share_start + jnp.arange(row_share, dtype=jnp.int32)
    field_of = global_cols // parallel_lines
    row_weights = latitude_weights(lat_first + global_cols % parallel_lines, parallel_number)
    row_scale = row_weights / (lon_total * lon_total * weight_total)
    weighted = powers.reshape(row_share, 3 * wave_count) * row_scale[:, None]
    field_index = jnp.arange(quantity_labels, dtype=jnp.int32)
    window = min(quantity_labels, row_share // parallel_lines + 2)
    first_field = share_start // parallel_lines
    window_index = jnp.arange(window, dtype=jnp.int32)
    offset = field_of - first_field
    selector = (offset[None, :] == window_index[:, None]).astype(jnp.float32)
    band_sum = jnp.dot(
        selector, weighted, precision=lax.Precision.HIGHEST, preferred_element_type=jnp.float32
    )
    band_sum = gathered_total(band_sum, LAT)
    gathered = gather_directly(band_sum, LON, 0)
    slot_index = jnp.arange(lon_devices * window, dtype=jnp.int32)
    slot_field = slot_index // window * row_share // parallel_lines + slot_index % window
    placer = (slot_field[None, :] == field_index[:, None]).astype(jnp.float32)
    summed = jnp.dot(
        placer, gathered, precision=lax.Precision.HIGHEST, preferred_element_type=jnp.float32
    )
    energy_curves = summed.reshape(quantity_labels, 3, wave_count).transpose(1, 0, 2)
    skill_means = one_axis_at_a_time(skill_terms, LAT_LON) / (lon_total * weight_total)
    rms_error = jnp.sqrt(skill_means[0])
    anomaly_corr = skill_means[1] / jnp.sqrt(
        (skill_means[2] + epsilon) * (skill_means[3] + epsilon)
    )
    return (energy_curves, rms_error, anomaly_corr)


def solution(mesh):
    split = Mesh(mesh.devices.reshape(8, 2, 4, 4), ("lat_0", "lat_1", "lon_0", "lon_1"))
    placed = (P(LON, LAT), P(LON, LAT), P(LON, LAT))
    return jax.shard_map(
        local, mesh=split, in_specs=placed, out_specs=(P(), P(), P()), check_vma=False
    )
```

profile of v0, /device:TPU:32, one launch (start us, length us, event | category | flops | bytes accessed | tf_op | source)
XLA Modules:
  0.0 134.7 jit_solution(8553598475362706822)
XLA Ops:
  0.6 1.4 %copy.28 = f32[90,1664]{0,1:T(8,128)S(1)} copy(f32[90,1664]{1,0:T(8,128)} %param.4) | data formatting | bytes 1198080 | tf_op args[1]
  2.0 0.1 reshape.127
  2.1 0.2 copy.29
  2.3 1.2 copy.30
  3.5 7.2 %all-to-all-start.1 = ((f32[90,16,104]{2,0,1:T(8,128)}), f32[90,16,104]{2,0,1:T(8,128)S(1)}, u32[]{:S(2)}, u32[]{:S(2)}) async-start(f32[90,16,104]{2,0,1:T(8,128)} %copy.30), calls=%async_computation.1 | async-start | bytes 1572864 | tf_op jit(solution)/shard_map/all_to_all | solution.py:116
  10.7 1.4 %copy.24 = f32[90,1664]{0,1:T(8,128)S(1)} copy(f32[90,1664]{1,0:T(8,128)} %param.3) | data formatting | bytes 1198080 | tf_op args[0]
  12.1 0.1 reshape.126
  12.1 0.2 copy.25
  12.3 1.3 copy.26
  13.6 0.1 mul.178
  13.7 0.1 mul.179
  13.8 0.6 cosine_reduce_fusion
  15.1 0.1 fusion.39
  15.2 0.0 copy-done
  15.2 1.6 %fusion.17 = (f32[1664]{0:T(1024)S(1)}, f32[1664]{0:T(1024)S(1)}, f32[1664]{0:T(1024)S(1)}, f32[1664]{0:T(1024)S(1)}) fusion(f32[90,1664]{1,0:T(8,128)} %param.3, f32[90,1664]{1,0:T(8,128)S(1)} %copy-done, f32[1664]{0:T(1024)S(1)} %mul.179, f32[90,1664]{1,0:T(8,128)} %param.5), kind=kLoop, calls=%fused_computation.27 | loop fusion | flops 2089984 | bytes 1830400 | tf_op jit(solution)/shard_map/reduce_sum | solution.py:102
  16.8 8.3 %all-to-all-done.1 = f32[90,16,104]{2,0,1:T(8,128)S(1)} async-done(((f32[90,16,104]{2,0,1:T(8,128)}), f32[90,16,104]{2,0,1:T(8,128)S(1)}, u32[]{:S(2)}, u32[]{:S(2)}) %all-to-all-start.1) | async-done | bytes 599072 | tf_op jit(solution)/shard_map/all_to_all | solution.py:116
  25.2 3.6 %all-to-all-start = ((f32[90,16,104]{2,0,1:T(8,128)}), f32[90,16,104]{2,0,1:T(8,128)S(1)}, u32[]{:S(2)}, u32[]{:S(2)}) async-start(f32[90,16,104]{2,0,1:T(8,128)} %copy.26), calls=%async_computation | async-start | bytes 1572864 | tf_op jit(solution)/shard_map/all_to_all | solution.py:115
  28.8 0.1 reduce_sum.94
  28.9 0.1 reduce_sum.91
  29.0 0.1 reduce_sum.88
  29.2 0.1 reduce_sum.68
  30.0 19.7 %sine_negate_fusion = (f32[1440,721]{1,0:T(8,128)}, f32[1440,721]{1,0:T(8,128)}) fusion(), kind=kLoop, calls=%fused_computation.7 | loop fusion | flops 10382400 | bytes 8305920 | tf_op jit(solution)/shard_map/neg | solution.py:52
  49.7 0.1 reshape.136
  49.7 0.3 copy.35
  50.0 0.0 all-to-all-done
  50.0 0.1 reshape.135
  50.0 0.3 copy.34
  50.3 10.6 %fusion = f32[208,1442]{1,0:T(8,128)S(1)} fusion(f32[1440,721]{1,0:T(8,128)} %get-tuple-element.11, f32[1440,721]{1,0:T(8,128)} %get-tuple-element.12, f32[1440,104]{0,1:T(8,128)S(1)} %copy.35, f32[1440,104]{0,1:T(8,128)S(1)} %copy.34), kind=kOutput, calls=%fused_computation | convolution fusion | flops 5185270272 | bytes 10703744 | tf_op jit(solution)/shard_map/dot_general | solution.py:56
  61.0 0.1 slice_subtract_fusion
  61.0 0.2 fusion.25
  61.3 0.2 fusion.21
  61.4 0.1 pad_maximum_fusion
  61.5 0.4 copy.32
  61.9 0.1 reshape.128
  62.0 0.7 convolution_bitcast_fusion
  62.7 21.0 %all-gather.1 = f32[16,5,2163]{2,1,0:T(8,128)S(1)} all-gather(f32[1,5,2163]{2,1,0:T(8,128)S(1)} %convolution_bitcast_fusion), channel_id=2, replica_groups=mesh['lat_0'=8,'lat_1'=2,'lon_0'=4,'lon_1'=4] {'lat_0','lat_1'}, dimensions={0}, use_global_device_ids=true | all-gather | bytes 735420 | tf_op jit(solution)/shard_map/all_gather | solution.py:17
  83.7 0.1 reduce_sum.66
  83.8 1.1 broadcast_in_dim.2
  84.9 7.2 %all-to-all-start.2 = ((f32[16,5,2163]{2,1,0:T(8,128)}), f32[16,5,2163]{2,1,0:T(8,128)S(1)}, u32[]{:S(2)}, u32[]{:S(2)}) async-start(f32[16,5,2163]{2,1,0:T(8,128)} %broadcast_in_dim.2), calls=%async_computation.2 | async-start | bytes 2228224 | tf_op jit(solution)/shard_map/all_to_all | solution.py:23
  92.1 16.3 %psum.28 = f32[4,52]{1,0:T(4,128)S(1)} all-reduce(f32[4,52]{1,0:T(4,128)S(1)} %pad_maximum_fusion.1), channel_id=1, replica_groups=mesh['lat_0'=8,'lat_1'=2,'lon_0'=4,'lon_1'=4] {'lat_0'}, use_global_device_ids=true, to_apply=%region_10.11 | all-reduce | flops 208 | bytes 1664 | tf_op jit(solution)/shard_map/psum | solution.py:39
  108.4 2.5 %psum.29 = f32[4,52]{1,0:T(4,128)S(1)} all-reduce(f32[4,52]{1,0:T(4,128)S(1)} %psum.28), channel_id=1, replica_groups=mesh['lat_0'=8,'lat_1'=2,'lon_0'=4,'lon_1'=4] {'lat_1'}, use_global_device_ids=true, to_apply=%region_11.12 | all-reduce | flops 208 | bytes 1664 | tf_op jit(solution)/shard_map/psum | solution.py:39
  110.8 10.8 %psum.30 = f32[4,52]{1,0:T(4,128)S(1)} all-reduce(f32[4,52]{1,0:T(4,128)S(1)} %psum.29), channel_id=1, replica_groups=mesh['lat_0'=8,'lat_1'=2,'lon_0'=4,'lon_1'=4] {'lon_0'}, use_global_device_ids=true, to_apply=%region_12.13 | all-reduce | flops 208 | bytes 1664 | tf_op jit(solution)/shard_map/psum | solution.py:39
  121.7 10.4 %psum.31 = f32[4,52]{1,0:T(4,128)S(1)} all-reduce(f32[4,52]{1,0:T(4,128)S(1)} %psum.30), channel_id=1, replica_groups=mesh['lat_0'=8,'lat_1'=2,'lon_0'=4,'lon_1'=4] {'lon_1'}, use_global_device_ids=true, to_apply=%region_13.14 | all-reduce | flops 208 | bytes 1664 | tf_op jit(solution)/shard_map/psum | solution.py:39
  132.1 0.5 multiply_bitcast_fusion
  132.6 0.0 all-to-all-done.2
  132.6 0.1 reshape.129
  132.7 0.7 dot_general.16
  133.4 1.3 convolution_bitcast_fusion.1
  (10 shorter events, 0.2 us)
Async XLA Ops:
  3.5 11.7 %copy-start = (f32[90,1664]{1,0:T(8,128)S(1)}, f32[90,1664]{1,0:T(8,128)}, u32[]{:S(2)}) copy-start(f32[90,1664]{1,0:T(8,128)} %param.4) | copy-start | bytes 1797124
  3.5 21.7 %all-to-all-start.1 = ((f32[90,16,104]{2,0,1:T(8,128)}), f32[90,16,104]{2,0,1:T(8,128)S(1)}, u32[]{:S(2)}, u32[]{:S(2)}) async-start(f32[90,16,104]{2,0,1:T(8,128)} %copy.30), calls=%async_computation.1 | async-start | bytes 1572864 | tf_op jit(solution)/shard_map/all_to_all | solution.py:116
  25.2 24.8 %all-to-all-start = ((f32[90,16,104]{2,0,1:T(8,128)}), f32[90,16,104]{2,0,1:T(8,128)S(1)}, u32[]{:S(2)}, u32[]{:S(2)}) async-start(f32[90,16,104]{2,0,1:T(8,128)} %copy.26), calls=%async_computation | async-start | bytes 1572864 | tf_op jit(solution)/shard_map/all_to_all | solution.py:115
  84.9 47.7 %all-to-all-start.2 = ((f32[16,5,2163]{2,1,0:T(8,128)}), f32[16,5,2163]{2,1,0:T(8,128)S(1)}, u32[]{:S(2)}, u32[]{:S(2)}) async-start(f32[16,5,2163]{2,1,0:T(8,128)} %broadcast_in_dim.2), calls=%async_computation.2 | async-start | bytes 2228224 | tf_op jit(solution)/shard_map/all_to_all | solution.py:23
where the time goes:
time: 135 us
  blocking collectives  61 us (45%)
  other arithmetic  23.4 us (17%)
  starting transfers between devices  17.9 us (13%)
  matrix products  12.6 us (9%)
  local copies, waits for them, and re-layouts  9.22 us (7%)
  waiting for transfers between devices  8.32 us (6%)
  between operations  2.19 us (2%)
    psum x4, blocking collectives, one_axis_at_a_time(): value = lax.psum(value, axis)  40 us
    all_gather x1, blocking collectives, gathered_total(): tiles = lax.all_gather(value, axis)  21 us
    neg x1, other arithmetic, dft_table(): return jnp.concatenate([jnp.cos(angle), -jnp.sin(angle)], axis=1)  19.7 us
    dot_general x1, matrix products, transform_columns(): lax.dot_general(stacked, table, (((0,), (0,)), ((), ())), precision=lax.P...  10.6 us
    all_to_all x1, waiting for transfers between devices, local(): lax.all_to_all(true_blocks, LON, split_axis=1, concat_axis=0, tiled=True)  8.32 us
    all_to_all x1, starting transfers between devices, local(): lax.all_to_all(true_blocks, LON, split_axis=1, concat_axis=0, tiled=True)  7.17 us
    all_to_all x1, starting transfers between devices, copy_for_each(): return lax.all_to_all(copies, axis, split_axis=0, concat_axis=0, tiled=True)  7.15 us
    all_to_all x1, starting transfers between devices, local(): lax.all_to_all(fore_blocks, LON, split_axis=1, concat_axis=0, tiled=True)  3.61 us
  transfers between devices with their start and end apart: 3, of which 1 were waited for; matrix products, arithmetic and copies ran while one was open for 20% of the time, Pallas kernels for 0%

commit v1 on v0

v1 whole, which is shorter than its diff:
```python
import functools

import jax
import jax.numpy as jnp
import numpy as np
from jax import lax
from jax.experimental import pallas as pl
from jax.experimental.pallas import tpu as pltpu
from jax.sharding import Mesh
from jax.sharding import PartitionSpec as P

FIELDS = 52
NLON = 1440
NLAT = 512
BLOCKS = 16
BLOCK = NLON // BLOCKS
WAVES = NLON // 2 + 1
LAT_LINES = 32
COLS = FIELDS * LAT_LINES
SHARE = COLS // BLOCKS
WHOLE = 3
REST = 8
HEAD = 64
TAIL_ROWS = 56
ROWS = SHARE + TAIL_ROWS
LANES = 128
WIDE = 768
HALF = WIDE // 2
LAT = ("lat_0", "lat_1")
LON = ("lon_0", "lon_1")

epsilon = 1e-06


def out_wave(k0, lane):
    if k0 == 0:
        if lane < 46:
            return 16 * lane
        if lane < 91:
            return 8 + 16 * (lane - 46)
        return -1
    if lane < 90:
        k = k0 + 16 * lane
        return min(k, NLON - k)
    return -1


def dft_tables():
    table = np.zeros((8, 256, 256), np.float64)
    m = np.arange(BLOCK)
    re_row = np.where(m < HEAD, m, 128 + m - HEAD)
    im_row = np.where(m < HEAD, HEAD + m, 160 + m - HEAD)
    for lane in range(90):
        for k0 in range(1, 8):
            angle = 2.0 * np.pi * ((m * (k0 + 16 * lane)) % NLON) / NLON
            table[k0, re_row, lane] = np.cos(angle)
            table[k0, im_row, lane] = np.sin(angle)
            table[k0, re_row, 128 + lane] = -np.sin(angle)
            table[k0, im_row, 128 + lane] = np.cos(angle)
    for lane in range(91):
        angle = 2.0 * np.pi * ((m * out_wave(0, lane)) % NLON) / NLON
        rows = re_row if lane < 46 else im_row
        table[0, rows, lane] = np.cos(angle)
        table[0, rows, 128 + lane] = -np.sin(angle)
    full = table.astype(np.float32)
    high = full.astype(jnp.bfloat16)
    low = (table - high.astype(np.float64)).astype(np.float32).astype(jnp.bfloat16)
    return np.concatenate([high, low], axis=0)


def order_table():
    row = jnp.arange(8 * LANES, dtype=jnp.int32)
    k0, lane = row // LANES, row % LANES
    ahead = k0 + 16 * lane
    wave = jnp.where(lane < 90, jnp.minimum(ahead, NLON - ahead), -1)
    first = jnp.where(lane < 46, 16 * lane, jnp.where(lane < 91, 8 + 16 * (lane - 46), -1))
    wave = jnp.where(k0 == 0, first, wave)
    return (wave[:, None] == jnp.arange(WIDE, dtype=jnp.int32)[None, :]).astype(jnp.bfloat16)


def pack_kernel(fore_ref, true_ref, out_ref, head_ref, tail_ref):
    lane = lax.broadcasted_iota(jnp.int32, (8, LANES), 1)
    pad = jnp.zeros((96 - BLOCK, LANES), jnp.float32)
    for j in range(COLS // LANES):
        cols = slice(j * LANES, (j + 1) * LANES)
        head = jnp.concatenate([fore_ref[:HEAD, cols], true_ref[:HEAD, cols]], axis=0)
        head_ref[cols, :] = head.T
        tail = jnp.concatenate(
            [fore_ref[HEAD:, cols], pad, true_ref[HEAD:, cols], pad], axis=0
        )
        tail = jnp.concatenate([tail, tail], axis=0)
        tail_ref[cols, :] = tail.T

    def piece(ref, s, part):
        if part < 12:
            field = WHOLE * s + part // 4
            first = 8 * (part % 4)
        else:
            field = WHOLE * BLOCKS + s // 4
            first = 8 * (s % 4)
        return ref[pl.ds(first * FIELDS + field, 8, stride=FIELDS), :]

    for s in range(BLOCKS):
        for part in range(13):
            out_ref[s, 8 * part : 8 * part + 8, :] = piece(head_ref, s, part)
        for part in range(7):
            near = piece(tail_ref, s, part)
            far = piece(tail_ref, s, min(part + 7, 12))
            out_ref[s, SHARE + 8 * part : SHARE + 8 * part + 8, :] = jnp.where(lane < HEAD, near, far)


def pack(fore, true):
    return pl.pallas_call(
        pack_kernel,
        out_shape=jax.ShapeDtypeStruct((BLOCKS, ROWS, LANES), jnp.float32),
        in_specs=[pl.BlockSpec(memory_space=pltpu.VMEM)] * 2,
        out_specs=pl.BlockSpec(memory_space=pltpu.VMEM),
        scratch_shapes=[pltpu.VMEM((COLS, LANES), jnp.float32)] * 2,
        name="pack",
    )(fore, true)


def sixteen(x):
    half = float(np.sqrt(0.5))
    e = [x[j] + x[j + 8] for j in range(8)]
    o = [x[j] - x[j + 8] for j in range(8)]
    ee = [e[j] + e[j + 4] for j in range(4)]
    eo = [e[j] - e[j + 4] for j in range(4)]
    a, b = ee[0] + ee[2], ee[1] + ee[3]
    out = {0: (a + b, a - b), 4: (ee[0] - ee[2], ee[3] - ee[1])}
    s, d = half * (eo[1] + eo[3]), half * (eo[1] - eo[3])
    out[2] = (eo[0] + d, -(eo[2] + s))
    out[6] = (eo[0] - d, eo[2] - s)
    p = [o[j] - o[8 - j] for j in range(1, 4)]
    q = [o[j] + o[8 - j] for j in range(1, 4)]
    for k in (1, 3, 5, 7):
        re, im = o[0], -float(np.round(np.sin(np.pi * k / 2))) * o[4]
        for j in range(1, 4):
            re = re + float(np.cos(np.pi * j * k / 8)) * p[j - 1]
            im = im - float(np.sin(np.pi * j * k / 8)) * q[j - 1]
        out[k] = (re, im)
    return out


def spectrum_kernel(got_ref, weight_ref, skill_ref, table_ref, order_ref, out_ref, y_ref, rows_ref):
    def butterfly(i, _):
        rows = pl.ds(pl.multiple_of(i * 8, 8), 8)
        out = sixteen([got_ref[d, rows, :] for d in range(BLOCKS)])
        for k0 in range(8):
            y_ref[2 * k0, rows, :] = out[k0][0]
            y_ref[2 * k0 + 1, rows, :] = out[k0][1]
        return 0

    lax.fori_loop(0, ROWS // 8, butterfly, 0, unroll=2)
    lane_head = lax.broadcasted_iota(jnp.int32, (SHARE, LANES), 1) < 64
    lane_tail = lax.broadcasted_iota(jnp.int32, (TAIL_ROWS, LANES), 1) < 32
    weight = weight_ref[...]
    for k0 in range(8):
        re, im = y_ref[2 * k0, :SHARE, :], y_ref[2 * k0 + 1, :SHARE, :]
        fore_head = jnp.where(lane_head, re, pltpu.roll(im, 64, 1))
        true_head = jnp.where(lane_head, pltpu.roll(re, 64, 1), im)
        re, im = y_ref[2 * k0, SHARE:, :], y_ref[2 * k0 + 1, SHARE:, :]
        slots = [
            jnp.where(
                lane_tail,
                re if s == 0 else pltpu.roll(re, 128 - 32 * s, 1),
                im if s == 1 else pltpu.roll(im, (160 - 32 * s) % 128, 1),
            )
            for s in range(4)
        ]
        rest = SHARE - TAIL_ROWS
        heads = jnp.concatenate([fore_head, true_head], axis=0)
        tails = jnp.concatenate([slots[0], slots[2][:rest], slots[1], slots[3][:rest]], axis=0)
        z = jnp.concatenate([heads, tails], axis=1)
        high = z.astype(jnp.bfloat16)
        low = (z - high.astype(jnp.float32)).astype(jnp.bfloat16)
        t_high, t_low = table_ref[k0], table_ref[8 + k0]
        dot = functools.partial(jnp.dot, preferred_element_type=jnp.float32)
        coeffs = dot(high, t_high) + (dot(low, t_high) + dot(high, t_low))
        fore, true = coeffs[:SHARE], coeffs[SHARE:]
        for c, part in enumerate((fore, true, fore - true)):
            square = part * part
            power = (square[:, :LANES] + square[:, LANES:]) * weight
            for f in range(4):
                first, last = 32 * f, min(32 * f + 32, SHARE)
                rows_ref[4 * c + f : 4 * c + f + 1, k0 * LANES : (k0 + 1) * LANES] = jnp.sum(
                    power[first:last], axis=0, keepdims=True
                )
    rows = rows_ref[:12, :]
    high = rows.astype(jnp.bfloat16)
    left = rows - high.astype(jnp.float32)
    middle = left.astype(jnp.bfloat16)
    low = (left - middle.astype(jnp.float32)).astype(jnp.bfloat16)
    order = order_ref[...]
    dot = functools.partial(jnp.dot, preferred_element_type=jnp.float32)
    placed = dot(high, order) + (dot(middle, order) + dot(low, order))
    out_ref[0, :12, :] = placed[:, :HALF]
    out_ref[1, :12, :] = placed[:, HALF:]
    out_ref[0, 12:, :] = skill_ref[...]
    out_ref[1, 12:, :] = jnp.zeros((4, HALF), jnp.float32)


def spectrum(got, weight, skill, table, order):
    return pl.pallas_call(
        spectrum_kernel,
        out_shape=jax.ShapeDtypeStruct((2, 16, HALF), jnp.float32),
        in_specs=[pl.BlockSpec(memory_space=pltpu.VMEM)] * 5,
        out_specs=pl.BlockSpec(memory_space=pltpu.VMEM),
        scratch_shapes=[
            pltpu.VMEM((BLOCKS, ROWS, LANES), jnp.float32),
            pltpu.VMEM((16, 8 * LANES), jnp.float32),
        ],
        name="spectrum",
    )(got, weight, skill, table, order)


def latitude_weights(lat_index):
    return jnp.cos(jnp.pi * ((lat_index.astype(jnp.float32) + 0.5) / NLAT - 0.5))


def to_all(value, axis):
    copies = jnp.broadcast_to(value, (lax.axis_size(axis), *value.shape))
    return lax.all_to_all(copies, axis, split_axis=0, concat_axis=0, tiled=True)


def skill_sums(predicted_state, verified_state, normal_state, weights):
    predicted = predicted_state - normal_state
    observed = verified_state - normal_state
    mismatch = predicted_state - verified_state
    column = jnp.repeat(weights, FIELDS)
    terms = [
        jnp.sum(u * v, axis=0) * column
        for u, v in (
            (mismatch, mismatch),
            (predicted, observed),
            (predicted, predicted),
            (observed, observed),
        )
    ]
    return jnp.stack([t.reshape(LAT_LINES, FIELDS).sum(axis=0) for t in terms])


def local(predicted_state, verified_state, normal_state):
    lon = lax.axis_index(LON)
    core = lax.axis_index("lat_1")
    lat_first = lax.axis_index(LAT) * LAT_LINES
    swap = [(0, 1), (1, 0)]
    message = pack(predicted_state, verified_state)
    got = lax.all_to_all(message, LON, split_axis=0, concat_axis=0, tiled=True)

    weights = latitude_weights(lat_first + jnp.arange(LAT_LINES, dtype=jnp.int32))
    weight_total = jnp.sum(latitude_weights(jnp.arange(NLAT, dtype=jnp.int32)))
    row = jnp.arange(SHARE, dtype=jnp.int32)
    row_lat = jnp.where(row < WHOLE * LAT_LINES, row % LAT_LINES, 8 * (lon % 4) + row % 8)
    row_weight = latitude_weights(lat_first + row_lat) / (NLON * NLON * weight_total)
    row_weight = jnp.broadcast_to(row_weight[:, None], (SHARE, LANES))
    skill = skill_sums(predicted_state, verified_state, normal_state, weights)
    skill = jnp.pad(skill, ((0, 0), (0, HALF - FIELDS)))

    parts = spectrum(got, row_weight, skill, jnp.asarray(dft_tables()), order_table())
    mine = jnp.where(core == 0, parts[0], parts[1])
    theirs = jnp.where(core == 0, parts[1], parts[0])
    half = mine + lax.ppermute(theirs, "lat_1", swap)
    half = to_all(half, "lat_0").sum(axis=0)
    shares = to_all(half, LON)

    groups = shares[:, :12].reshape(BLOCKS, 3, 4, HALF).transpose(1, 0, 2, 3)
    whole = groups[:, :, :WHOLE].reshape(3, WHOLE * BLOCKS, HALF)
    rest = groups[:, :, WHOLE].reshape(3, 4, 4, HALF).sum(axis=2)
    sums = shares[:, 12:].sum(axis=0)
    mine = jnp.concatenate(
        [whole.reshape(-1, HALF), rest.reshape(-1, HALF), sums], axis=0
    )
    theirs = lax.ppermute(mine, "lat_1", swap)
    first = jnp.where(core == 0, mine, theirs)
    second = jnp.where(core == 0, theirs, mine)
    both = jnp.concatenate([first, second], axis=1)
    split = 3 * WHOLE * BLOCKS
    energy_curves = jnp.concatenate(
        [both[:split].reshape(3, -1, WIDE), both[split : split + 12].reshape(3, 4, WIDE)], axis=1
    )[:, :, :WAVES]
    means = first[split + 12 :, :FIELDS] / (NLON * weight_total)
    rms_error = jnp.sqrt(means[0])
    anomaly_corr = means[1] / jnp.sqrt((means[2] + epsilon) * (means[3] + epsilon))
    return energy_curves, rms_error, anomaly_corr


def solution(mesh):
    split = Mesh(mesh.devices.reshape(8, 2, 4, 4), ("lat_0", "lat_1", "lon_0", "lon_1"))
    placed = (P(LON, LAT), P(LON, LAT), P(LON, LAT))
    return jax.shard_map(
        local, mesh=split, in_specs=placed, out_specs=(P(), P(), P()), check_vma=False
    )
```

time: 135 us -> 77.5 us (0.57)
  the two profiles are of different devices: /device:TPU:32 before, /device:TPU:1 now
where the time goes in v1:
time: 77.5 us; the launch traced here: 77.1 us
  blocking collectives  28.5 us (37%)
  waiting for transfers between devices  16 us (21%)
  starting transfers between devices  14 us (18%)
  Pallas kernels  8.26 us (11%)
  other arithmetic  6.3 us (8%)
  between operations  2.13 us (3%)
  local copies, waits for them, and re-layouts  1.93 us (2%)
    all_to_all x2, blocking collectives, to_all(): return lax.all_to_all(copies, axis, split_axis=0, concat_axis=0, tiled=True)  28.5 us
    all_to_all x1, waiting for transfers between devices, local(): got = lax.all_to_all(message, LON, split_axis=0, concat_axis=0, tiled=True)  14.6 us
    all_to_all x1, starting transfers between devices, local(): got = lax.all_to_all(message, LON, split_axis=0, concat_axis=0, tiled=True)  7.7 us
    pallas_call x1, Pallas kernels, spectrum(): pl.pallas_call(spectrum_kernel, out_shape=jax.ShapeDtypeStruct((2, 16, HA...  5.32 us
    ppermute x1, starting transfers between devices, local(): theirs = lax.ppermute(mine, 'lat_1', swap)  3.36 us
    pallas_call x1, Pallas kernels, pack(): pl.pallas_call(pack_kernel, out_shape=jax.ShapeDtypeStruct((BLOCKS, ROWS,...  2.94 us
    ppermute x1, starting transfers between devices, local(): half = mine + lax.ppermute(theirs, 'lat_1', swap)  2.92 us
  transfers between devices with their start and end apart: 3, of which 3 were waited for; matrix products, arithmetic and copies ran while one was open for 5% of the time, Pallas kernels for 0%

profile of v1, /device:TPU:1, one launch (start us, length us, event | category | flops | bytes accessed | tf_op | source)
XLA Modules:
  0.0 77.1 jit_solution(11424822457836321808)
XLA Ops:
  0.6 2.9 %pack.1 = f32[16,160,128]{2,1,0:T(8,128)} custom-call(f32[90,1664]{1,0:T(8,128)} %fore_ref.1, f32[90,1664]{1,0:T(8,128)} %true_ref.1), custom_call_target="tpu_custom_call" | custom-call | tf_op jit(solution)/shard_map/pack/pallas_call | solution.py:113
  3.6 0.0 copy-start.1
  3.6 0.0 copy-start.2
  3.6 0.0 copy-start.3
  3.6 7.7 %all-to-all-start = ((f32[16,160,128]{2,1,0:T(8,128)}), f32[16,160,128]{2,1,0:T(8,128)S(1)}, u32[]{:S(2)}, u32[]{:S(2)}) async-start(f32[16,160,128]{2,1,0:T(8,128)} %pack.1), calls=%async_computation | async-start | bytes 2621440 | tf_op jit(solution)/shard_map/all_to_all | solution.py:249
  11.3 0.0 copy-done.1
  11.3 0.0 copy-done.2
  11.3 0.0 copy-done.3
  11.3 0.3 multiply_reduce_fusion.3
  11.6 0.1 reduce_sum.118
  11.7 0.1 reduce_sum.121
  11.8 0.1 reduce_sum.127
  11.9 0.1 reduce_sum.124
  12.0 0.6 cosine_reduce_fusion
  13.4 0.1 cosine_divide_fusion
  13.5 0.1 multiply_reduce_fusion.7
  13.6 0.6 select_maximum_fusion.skill_ref
  14.2 1.5 %fusion.order_ref = bf16[1024,768]{1,0:T(8,128)(2,1)} fusion(s32[1024]{0:T(1024)S(1)} %fusion.9), kind=kLoop, calls=%fused_computation.1 | loop fusion | flops 1572864 | bytes 1576960 | tf_op jit(solution)/shard_map/convert_element_type | solution.py:78
  15.6 14.6 %all-to-all-done.got_ref = f32[16,160,128]{2,1,0:T(8,128)S(1)} async-done(((f32[16,160,128]{2,1,0:T(8,128)}), f32[16,160,128]{2,1,0:T(8,128)S(1)}, u32[]{:S(2)}, u32[]{:S(2)}) %all-to-all-start) | async-done | bytes 1310752 | tf_op jit(solution)/shard_map/all_to_all | solution.py:249
  30.3 0.0 copy-start
  30.3 0.8 %broadcast_in_dim.20.weight_ref = f32[104,128]{1,0:T(8,128)} broadcast(f32[104]{0:T(128)S(1)} %cosine_divide_fusion), dimensions={0} | broadcast | bytes 53664 | tf_op jit(solution)/shard_map/broadcast_in_dim | solution.py:256
  31.1 0.3 copy-done
  31.3 5.3 %spectrum.1 = f32[2,16,384]{2,1,0:T(8,128)} custom-call(f32[16,160,128]{2,1,0:T(8,128)} %copy-done, f32[104,128]{1,0:T(8,128)} %broadcast_in_dim.20.weight_ref, f32[4,384]{1,0:T(4,128)} %select_maximum_fusion.skill_ref, bf16[16,256,256]{2,1,0:T(8,128)(2,1)} %constant.138.clone.table_ref, bf16[1024,768]{1,0:T(8,128)(2,1)} %fusion.order_ref), custom_call_target="tpu_custom_call" | custom-call | tf_op jit(solution)/shard_map/spectrum/pallas_call | solution.py:204
  36.7 0.8 select_bitcast_fusion
  37.4 2.9 %collective-permute-start = (f32[16,384]{1,0:T(8,128)S(1)}, f32[16,384]{1,0:T(8,128)S(1)}, u32[]{:S(2)}, u32[]{:S(2)}) collective-permute-start(f32[16,384]{1,0:T(8,128)S(1)} %select_bitcast_fusion), channel_id=1, source_target_pairs={{0,16},{16,0},{1,17},{17,1},{2,18},{18,2},{3,19},{19,3},{4,20},{20... | collective-permute-start | bytes 73736 | tf_op jit(solution)/shard_map/ppermute | solution.py:263
  40.3 0.8 %collective-permute-done = f32[16,384]{1,0:T(8,128)S(1)} collective-permute-done((f32[16,384]{1,0:T(8,128)S(1)}, f32[16,384]{1,0:T(8,128)S(1)}, u32[]{:S(2)}, u32[]{:S(2)}) %collective-permute-start) | collective-permute-done | bytes 24608 | tf_op jit(solution)/shard_map/ppermute | solution.py:263
  41.2 0.8 bitcast_add_fusion
  42.0 17.4 %all_to_all.15 = f32[8,16,384]{2,1,0:T(8,128)S(1)} all-to-all(f32[8,16,384]{2,1,0:T(8,128)S(1)} %broadcast_in_dim.22), channel_id=1, replica_groups=mesh['lat_0'=8,'lat_1'=2,'lon_0'=4,'lon_1'=4] {'lat_0'}, dimensions={0} | all-to-all | bytes 393216 | tf_op jit(solution)/shard_map/all_to_all | solution.py:223
  59.5 11.1 %all_to_all.16 = f32[16,16,384]{2,1,0:T(8,128)S(1)} all-to-all(f32[16,16,384]{2,1,0:T(8,128)S(1)} %broadcast_in_dim.23), channel_id=1, replica_groups=mesh['lat_0'=8,'lat_1'=2,'lon_0'=4,'lon_1'=4] {'lon_0','lon_1'}, dimensions={0} | all-to-all | bytes 786432 | tf_op jit(solution)/shard_map/all_to_all | solution.py:223
  70.5 0.1 copy.12
  70.7 0.1 reduce_sum.130
  70.8 0.1 copy.11
  70.9 0.1 reshape_reshape.3
  71.1 3.4 %collective-permute-start.1 = (f32[160,384]{1,0:T(8,128)S(1)}, f32[160,384]{1,0:T(8,128)S(1)}, u32[]{:S(2)}, u32[]{:S(2)}) collective-permute-start(f32[160,384]{1,0:T(8,128)S(1)} %pad_maximum_fusion.1), channel_id=1, source_target_pairs={{0,16},{16,0},{1,17},{17,1},{2,18},{18,2},{3,19},{19,3},{4,20},{20... | collective-permute-start | bytes 737288 | tf_op jit(solution)/shard_map/ppermute | solution.py:274
  75.1 0.5 collective-permute-done.1
  75.7 0.5 multiply_bitcast_fusion
  76.3 0.8 %pad_maximum_fusion = f32[3,52,721]{2,1,0:T(8,128)} fusion(f32[3,4,768]{2,1,0:T(4,128)S(1)} %reshape.105, f32[3,48,768]{2,1,0:T(8,128)S(1)} %bitcast.22), kind=kLoop, calls=%fused_computation.6 | loop fusion | flops 112476 | bytes 929136 | tf_op jit(solution)/shard_map/concatenate | solution.py:279
  (16 shorter events, 0.3 us)
Async XLA Ops:
  3.6 7.7 %copy-start.1 = (f32[90,1664]{1,0:T(8,128)S(1)}, f32[90,1664]{1,0:T(8,128)}, u32[]{:S(2)}) copy-start(f32[90,1664]{1,0:T(8,128)} %fore_ref.1) | copy-start | bytes 1797124
  3.6 7.7 %copy-start.2 = (f32[90,1664]{1,0:T(8,128)S(1)}, f32[90,1664]{1,0:T(8,128)}, u32[]{:S(2)}) copy-start(f32[90,1664]{1,0:T(8,128)} %true_ref.1) | copy-start | bytes 1797124
  3.6 7.8 %copy-start.3 = (f32[90,1664]{1,0:T(8,128)S(1)}, f32[90,1664]{1,0:T(8,128)}, u32[]{:S(2)}) copy-start(f32[90,1664]{1,0:T(8,128)} %param.6) | copy-start | bytes 1797124
  3.6 26.7 %all-to-all-start = ((f32[16,160,128]{2,1,0:T(8,128)}), f32[16,160,128]{2,1,0:T(8,128)S(1)}, u32[]{:S(2)}, u32[]{:S(2)}) async-start(f32[16,160,128]{2,1,0:T(8,128)} %pack.1), calls=%async_computation | async-start | bytes 2621440 | tf_op jit(solution)/shard_map/all_to_all | solution.py:249
  30.3 1.1 %copy-start = (f32[16,160,128]{2,1,0:T(8,128)}, f32[16,160,128]{2,1,0:T(8,128)S(1)}, u32[]{:S(2)}) copy-start(f32[16,160,128]{2,1,0:T(8,128)S(1)} %all-to-all-done.got_ref) | copy-start | bytes 3932164
  37.4 3.8 %collective-permute-start = (f32[16,384]{1,0:T(8,128)S(1)}, f32[16,384]{1,0:T(8,128)S(1)}, u32[]{:S(2)}, u32[]{:S(2)}) collective-permute-start(f32[16,384]{1,0:T(8,128)S(1)} %select_bitcast_fusion), channel_id=1, source_target_pairs={{0,16},{16,0},{1,17},{17,1},{2,18},{18,2},{3,19},{19,3},{4,20},{20... | collective-permute-start | bytes 73736 | tf_op jit(solution)/shard_map/ppermute | solution.py:263
  71.1 4.5 %collective-permute-start.1 = (f32[160,384]{1,0:T(8,128)S(1)}, f32[160,384]{1,0:T(8,128)S(1)}, u32[]{:S(2)}, u32[]{:S(2)}) collective-permute-start(f32[160,384]{1,0:T(8,128)S(1)} %pad_maximum_fusion.1), channel_id=1, source_target_pairs={{0,16},{16,0},{1,17},{17,1},{2,18},{18,2},{3,19},{19,3},{4,20},{20... | collective-permute-start | bytes 737288 | tf_op jit(solution)/shard_map/ppermute | solution.py:274
